TPU v7x, 32 devices: a whole 2x2x4 slice. The times are simulated.
32 devices in a mesh: text: 16 (over z, y, x), query: 2 (over core).
Axes of the slice: x: 2, y: 2, z: 4, core: 2. Of those that a mesh axis runs over, the one named last changes fastest.
Arguments:
- query_embed: bfloat16 [1024, 1024], P(('text', 'query')), may hold values from -6 to 6
- truth_ids: int32 [1024], P(('text', 'query')), may hold values from 0 to 8191
- text_embed: bfloat16 [8192, 1024], P('text'), may hold values from -0.1875 to 0.1875
- text_ids: int32 [8192], P('text'), may hold values from 0 to 8191, each once
Outputs:
- top_scores: float32 [1024, 10], P(('text', 'query'))
- margins: float32 [1024, 3], P(('text', 'query'))
Inputs may be any that keep to these rules, and one draw needn't show every extreme that they name: `text_ids`: every id of 0 to 8191 stands in exactly one row.
All inputs are finite; a program needn't handle non-finite values.
Results may differ from a plain program's by a relative error of at most 0.0003.
Values may be sent and summed in bfloat16 or wider, within the bound.
No kernel may reach another device: no remote copies, remote signals or barrier semaphores. Data moves between devices by JAX's collectives and lax.ppermute only.
A program may use at most 64 MiB of HBM per device.

v0:
```python
import jax
import jax.numpy as jnp
from jax import lax
from jax.sharding import PartitionSpec as P

TOPK = 10


def per_device(query_embed, truth_ids, text_embed, text_ids):
    position = lax.axis_index("text")
    own_rows = query_embed.shape[0]
    gathered = lax.all_gather(query_embed, "text", axis=0, tiled=True)
    wanted = lax.all_gather(truth_ids, "text", axis=0, tiled=True)
    row_count = gathered.shape[0]
    block_rows = min(512, row_count)
    block_count = row_count // block_rows

    def score_block(operand):
        query_slab, wanted_ids = operand
        scores = lax.dot_general(
            query_slab, text_embed, (((1,), (1,)), ((), ())), preferred_element_type=jnp.float32
        )
        leaders = lax.top_k(scores, TOPK)[0]
        truth_part = jnp.sum(
            jnp.where(text_ids[None, :] == wanted_ids[:, None], scores, 0.0), axis=1
        )
        return (leaders, truth_part)

    leaders, truth_part = lax.map(
        score_block,
        (
            gathered.reshape(block_count, block_rows, gathered.shape[1]),
            wanted.reshape(block_count, block_rows),
        ),
    )
    leaders = leaders.reshape(row_count, TOPK)
    truth_part = truth_part.reshape(row_count)
    pooled = lax.all_to_all(leaders, "text", split_axis=0, concat_axis=1, tiled=True)
    chosen = lax.top_k(pooled, TOPK)[0]
    summed = lax.psum(truth_part, "text")
    truth_score = lax.dynamic_slice_in_dim(summed, position * own_rows, own_rows, 0)
    margins = jnp.stack(
        [truth_score - chosen[:, 0], truth_score - chosen[:, 4], truth_score - chosen[:, 9]], axis=1
    )
    return (chosen, margins)


def solution(mesh):
    return jax.shard_map(
        per_device,
        mesh=mesh,
        in_specs=(P(("text", "query"), None), P(("text", "query")), P("text", None), P("text")),
        out_specs=(P(("text", "query"), None), P(("text", "query"), None)),
        check_vma=False,
    )
```

profile of v0, /device:TPU:0, one launch (start us, length us, event | category | flops | bytes accessed | tf_op | source)
XLA Modules:
  0.0 162.6 jit_solution(6516423527075687639)
XLA Ops:
  7.2 0.0 copy-start
  7.2 0.0 all-gather.2.cloned.1.call-start
  7.2 0.7 all-gather.2.cloned.1.call-update
  7.9 0.0 copy-start.3
  7.9 0.6 copy-done.3
  8.6 0.6 dynamic-slice.2
  9.8 0.0 copy-start.2
  9.8 0.6 copy-done.2
  10.5 0.2 dynamic-update-slice
  10.7 0.0 copy-start.1
  10.7 16.3 %all-reduce = s32[512]{0:T(512)S(1)} all-reduce(s32[512]{0:T(512)S(1)} %dynamic-update-slice), channel_id=1, replica_groups=mesh['text'=16,'query'=2] {'text'}, use_global_device_ids=true, to_apply=%add | all-reduce | flops 512 | bytes 4096
  27.0 41.6 %all-gather.2.cloned.1.call-done = bf16[512,1024]{1,0:T(8,128)(2,1)} async-done(((bf16[32,1024]{1,0:T(8,128)(2,1)}), bf16[512,1024]{1,0:T(8,128)(2,1)}) %all-gather.2.cloned.1.call-update) | async-done | bytes 1048592 | tf_op jit(solution)/shard_map/all_gather | solution.py:12
  68.6 0.0 copy-done
  68.6 0.0 copy-done.1
  68.6 2.0 %select_reduce_fusion = (f32[512]{0:T(512)S(1)}, f32[512,512]{0,1:T(8,128)S(1)}) fusion(s32[512]{0:T(512)S(1)} %all-reduce, s32[512]{0:T(512)S(1)} %copy-done.1, bf16[512,1024]{1,0:T(8,128)(2,1)} %all-gather.2.cloned.1.call-done, bf16[512,1024]{1,0:T(8,128)(2,1)S(1)} %copy-done), kind=kOutput, calls=%fused_computation | convolution fusion | flops 537656832 | bytes 3151872 | tf_op jit(solution)/shard_map/while/body/eval_jaxpr/dot_general | solution.py:20
  70.6 0.1 iota.6.clone
  70.7 29.4 %top_k.14 = (f32[512,512]{0,1:T(8,128)}, s32[512,512]{0,1:T(8,128)}) sort(f32[512,512]{0,1:T(8,128)S(1)} %get-tuple-element.42, s32[512,512]{0,1:T(8,128)S(1)} %iota.6.clone), dimensions={1}, to_apply=%region_0.1 | sort | flops 4718592 | bytes 4194304 | tf_op jit(solution)/shard_map/while/body/eval_jaxpr/top_k | solution.py:23
  100.0 1.6 copy.16
  101.6 0.2 copy.11
  101.8 0.7 reshape.28
  102.5 4.5 %all-to-all-start = ((f32[16,1,320]{2,1,0:T(1,128)}), f32[16,1,320]{2,1,0:T(1,128)S(1)}, u32[]{:S(2)}, u32[]{:S(2)}) async-start(f32[16,1,320]{2,1,0:T(1,128)} %reshape.28), calls=%async_computation | async-start | bytes 49152 | tf_op jit(solution)/shard_map/all_to_all | solution.py:38
  107.0 42.1 %psum.7 = f32[512]{0:T(512)S(1)} all-reduce(f32[512]{0:T(512)S(1)} %get-tuple-element.41), channel_id=1, replica_groups=mesh['text'=16,'query'=2] {'text'}, use_global_device_ids=true, to_apply=%region_3.4 | all-reduce | flops 512 | bytes 4096 | tf_op jit(solution)/shard_map/psum | solution.py:40
  149.1 0.0 all-to-all-done
  149.1 0.5 broadcast.12
  149.6 0.7 reduce.6
  150.3 0.1 reshape.29
  150.4 0.1 copy.12
  150.5 3.8 %top_k.20 = (f32[32,160]{1,0:T(8,128)S(1)}, s32[32,160]{1,0:T(8,128)}) sort(f32[32,160]{1,0:T(8,128)S(1)} %copy.12, s32[32,160]{1,0:T(8,128)S(1)} %iota.7), dimensions={1}, to_apply=%region_1.2 | sort | flops 66560 | bytes 81920 | tf_op jit(solution)/shard_map/top_k | solution.py:39
  154.3 0.2 slice_reduce_fusion.2
  154.5 0.7 copy.13
  155.1 0.1 subtract_bitcast_fusion.2
  155.2 0.6 pad_maximum_fusion
  (6 shorter events, 0.1 us)
Async XLA Ops:
  7.2 61.4 %copy-start = (bf16[512,1024]{1,0:T(8,128)(2,1)S(1)}, bf16[512,1024]{1,0:T(8,128)(2,1)}, u32[]{:S(2)}) copy-start(bf16[512,1024]{1,0:T(8,128)(2,1)} %param.6) | copy-start | bytes 3145732
  7.2 61.4 %all-gather.2.cloned.1.call-start = ((), (), s32[]{:S(2)}) async-start(), calls=%async_computation.1 | async-start | bytes 1114112 | tf_op jit(solution)/shard_map/all_gather | solution.py:12
  7.9 0.7 copy-start.3
  9.8 0.7 copy-start.2
  10.7 57.9 %copy-start.1 = (s32[512]{0:T(512)S(1)}, s32[512]{0:T(512)}, u32[]{:S(2)}) copy-start(s32[512]{0:T(512)} %param.7) | copy-start | bytes 6148
  102.5 46.5 %all-to-all-start = ((f32[16,1,320]{2,1,0:T(1,128)}), f32[16,1,320]{2,1,0:T(1,128)S(1)}, u32[]{:S(2)}, u32[]{:S(2)}) async-start(f32[16,1,320]{2,1,0:T(1,128)} %reshape.28), calls=%async_computation | async-start | bytes 49152 | tf_op jit(solution)/shard_map/all_to_all | solution.py:38
Sparse Core Ops, SparseCore 0:
  10.7 57.7 all-gather.1
where the time goes:
time: 163 us
  blocking collectives  58.4 us (36%)
  waiting for transfers between devices  42.3 us (26%)
  other arithmetic  34.5 us (21%)
  between operations  14.8 us (9%)
  local copies, waits for them, and re-layouts  6.15 us (4%)
  starting transfers between devices  4.49 us (3%)
  matrix products  1.98 us (1%)
    psum x1, blocking collectives, per_device(): summed = lax.psum(truth_part, 'text')  42.1 us
    all_gather x1, waiting for transfers between devices, per_device(): gathered = lax.all_gather(query_embed, 'text', axis=0, tiled=True)  41.6 us
    top_k x1, other arithmetic, score_block(): leaders = lax.top_k(scores, TOPK)[0]  29.4 us
    unnamed x1, blocking collectives  16.3 us
    all_to_all x1, starting transfers between devices, per_device(): lax.all_to_all(leaders, 'text', split_axis=0, concat_axis=1, tiled=True)  4.45 us
    top_k x1, other arithmetic, per_device(): chosen = lax.top_k(pooled, TOPK)[0]  3.78 us
    unnamed x14, local copies, waits for them, and re-layouts  3.54 us
  transfers between devices with their start and end apart: 2, of which 1 were waited for; matrix products, arithmetic and copies ran while one was open for 0% of the time, Pallas kernels for 0%

commit v1 on v0

--- a/solution.py
+++ b/solution.py
@@ -6,10 +6,22 @@
 TOPK = 10
 
 
+def collect(x, axis, dim):
+    ways, here = (lax.axis_size(axis), lax.axis_index(axis))
+    grown, reach = (x, 1)
+    while reach < ways:
+        theirs = lax.ppermute(grown, axis, [(d, d ^ reach) for d in range(ways)])
+        mine_first = jnp.concatenate([grown, theirs], axis=dim)
+        theirs_first = jnp.concatenate([theirs, grown], axis=dim)
+        grown = jnp.where(here & reach == 0, mine_first, theirs_first)
+        reach = 2 * reach
+    return grown
+
+
 def per_device(query_embed, truth_ids, text_embed, text_ids):
     position = lax.axis_index("text")
     own_rows = query_embed.shape[0]
-    gathered = lax.all_gather(query_embed, "text", axis=0, tiled=True)
+    gathered = collect(query_embed, "text", 0)
     wanted = lax.all_gather(truth_ids, "text", axis=0, tiled=True)
     row_count = gathered.shape[0]
     block_rows = min(512, row_count)

time: 163 us -> 132 us (0.81)
  waiting for transfers between devices: 42.3 us -> 9.76 us
  starting transfers between devices: 4.49 us -> 18.1 us
  between operations: 14.8 us -> 1.45 us
    all_gather x1 -> x0, waiting for transfers between devices: 41.6 us -> none  [per_device(): gathered = lax.all_gather(query_embed, 'text', axis=0, tiled=True)]
    ppermute x0 -> x4, starting transfers between devices: none -> 11.3 us  [collect(): theirs = lax.ppermute(grown, axis, [(d, d ^ reach) for d in range(ways)])]
    ppermute x0 -> x4, waiting for transfers between devices: none -> 9.76 us  [collect(): theirs = lax.ppermute(grown, axis, [(d, d ^ reach) for d in range(ways)])]
    all_to_all x1, starting transfers between devices: 4.45 us -> 6.8 us  [per_device(): lax.all_to_all(leaders, 'text', split_axis=0, concat_axis=1, tiled=True)]
  transfers between devices with their start and end apart: 2 -> 5, of which waited for: 1 -> 3; matrix products, arithmetic and copies ran while one was open for 0% -> 1% of each run, Pallas kernels for 0% -> 0%
where the time goes in v1:
time: 132 us; the launch traced here: 131 us
  blocking collectives  59.6 us (45%)
  other arithmetic  35.6 us (27%)
  starting transfers between devices  18.1 us (14%)
  waiting for transfers between devices  9.76 us (7%)
  local copies, waits for them, and re-layouts  4.93 us (4%)
  matrix products  1.97 us (1%)
  between operations  1.45 us (1%)
    psum x1, blocking collectives, per_device(): summed = lax.psum(truth_part, 'text')  42.1 us
    top_k x1, other arithmetic, score_block(): leaders = lax.top_k(scores, TOPK)[0]  29.4 us
    unnamed x1, blocking collectives  17.5 us
    ppermute x4, starting transfers between devices, collect(): theirs = lax.ppermute(grown, axis, [(d, d ^ reach) for d in range(ways)])  11.3 us
    ppermute x4, waiting for transfers between devices, collect(): theirs = lax.ppermute(grown, axis, [(d, d ^ reach) for d in range(ways)])  9.76 us
    all_to_all x1, starting transfers between devices, per_device(): lax.all_to_all(leaders, 'text', split_axis=0, concat_axis=1, tiled=True)  6.8 us
    top_k x1, other arithmetic, per_device(): chosen = lax.top_k(pooled, TOPK)[0]  3.78 us
  transfers between devices with their start and end apart: 5, of which 3 were waited for; matrix products, arithmetic and copies ran while one was open for 1% of the time, Pallas kernels for 0%

profile of v1, /device:TPU:0, one launch (start us, length us, event | category | flops | bytes accessed | tf_op | source)
XLA Modules:
  0.0 131.5 jit_solution(18005538857997733873)
XLA Ops:
  0.6 0.0 copy-start
  0.6 0.0 copy-start.3
  0.7 3.0 %collective-permute-start = (bf16[32,1024]{1,0:T(8,128)(2,1)}, bf16[32,1024]{1,0:T(8,128)(2,1)S(1)}, u32[]{:S(2)}, u32[]{:S(2)}) collective-permute-start(bf16[32,1024]{1,0:T(8,128)(2,1)} %param.4), channel_id=1, source_target_pairs={{0,2},{2,0},{4,6},{6,4},{8,10},{10,8},{12,14},{14,12},{16,18},{18,... | collective-permute-start | bytes 196616 | tf_op jit(solution)/shard_map/ppermute | solution.py:13
  3.7 2.5 %collective-permute-done = bf16[32,1024]{1,0:T(8,128)(2,1)S(1)} collective-permute-done((bf16[32,1024]{1,0:T(8,128)(2,1)}, bf16[32,1024]{1,0:T(8,128)(2,1)S(1)}, u32[]{:S(2)}, u32[]{:S(2)}) %collective-permute-start) | collective-permute-done | bytes 65568 | tf_op jit(solution)/shard_map/ppermute | solution.py:13
  6.2 0.9 maximum_select_fusion.4
  7.1 2.1 %collective-permute-start.1 = (bf16[64,1024]{1,0:T(8,128)(2,1)S(1)}, bf16[64,1024]{1,0:T(8,128)(2,1)S(1)}, u32[]{:S(2)}, u32[]{:S(2)}) collective-permute-start(bf16[64,1024]{1,0:T(8,128)(2,1)S(1)} %maximum_select_fusion.4), channel_id=1, source_target_pairs={{0,4},{2,6},{4,0},{6,2},{8,12},{10,14},{12,8},{14,10},{16,20},{18,... | collective-permute-start | bytes 393224 | tf_op jit(solution)/shard_map/ppermute | solution.py:13
  9.2 2.9 %collective-permute-done.1 = bf16[64,1024]{1,0:T(8,128)(2,1)S(1)} collective-permute-done((bf16[64,1024]{1,0:T(8,128)(2,1)S(1)}, bf16[64,1024]{1,0:T(8,128)(2,1)S(1)}, u32[]{:S(2)}, u32[]{:S(2)}) %collective-permute-start.1) | collective-permute-done | bytes 131104 | tf_op jit(solution)/shard_map/ppermute | solution.py:13
  12.2 2.1 %collective-permute-start.2 = (bf16[128,1024]{1,0:T(8,128)(2,1)S(1)}, bf16[128,1024]{1,0:T(8,128)(2,1)S(1)}, u32[]{:S(2)}, u32[]{:S(2)}) collective-permute-start(bf16[128,1024]{1,0:T(8,128)(2,1)S(1)} %maximum_select_fusion.3), channel_id=1, source_target_pairs={{0,8},{2,10},{4,12},{6,14},{8,0},{10,2},{12,4},{14,6},{16,24},{18,... | collective-permute-start | bytes 786440 | tf_op jit(solution)/shard_map/ppermute | solution.py:13
  14.4 4.4 %collective-permute-done.2 = bf16[128,1024]{1,0:T(8,128)(2,1)S(1)} collective-permute-done((bf16[128,1024]{1,0:T(8,128)(2,1)S(1)}, bf16[128,1024]{1,0:T(8,128)(2,1)S(1)}, u32[]{:S(2)}, u32[]{:S(2)}) %collective-permute-start.2) | collective-permute-done | bytes 262176 | tf_op jit(solution)/shard_map/ppermute | solution.py:13
  18.7 0.1 maximum_select_fusion.2
  18.9 4.0 %collective-permute-start.3 = (bf16[256,1024]{1,0:T(8,128)(2,1)S(1)}, bf16[256,1024]{1,0:T(8,128)(2,1)}, u32[]{:S(2)}, u32[]{:S(2)}) collective-permute-start(bf16[256,1024]{1,0:T(8,128)(2,1)S(1)} %maximum_select_fusion.2), channel_id=1, source_target_pairs={{0,16},{2,18},{4,20},{6,22},{8,24},{10,26},{12,28},{14,30},{16,0},... | collective-permute-start | bytes 1572872 | tf_op jit(solution)/shard_map/ppermute | solution.py:13
  22.9 0.6 dynamic-slice.2
  24.1 0.2 dynamic-update-slice
  24.4 17.5 %all-reduce = s32[512]{0:T(512)S(1)} all-reduce(s32[512]{0:T(512)S(1)} %dynamic-update-slice), channel_id=1, replica_groups=mesh['text'=16,'query'=2] {'text'}, use_global_device_ids=true, to_apply=%add | all-reduce | flops 512 | bytes 4096
  41.9 0.0 collective-permute-done.3
  41.9 2.0 %select_reduce_fusion = (f32[512]{0:T(512)S(1)}, f32[512,512]{0,1:T(8,128)S(1)}) fusion(s32[512]{0:T(512)S(1)} %all-reduce, s32[512]{0:T(512)S(1)} %copy-done.1, bf16[512,1024]{1,0:T(8,128)(2,1)S(1)} %copy-done, bf16[256,1024]{1,0:T(8,128)(2,1)} %collective-permute-done.3, bf16[256,1024]{1,0:T(8,128)(2,1)S(1)} %maximum_select_fusion.2, pred[]{:T(512)S(6)} %eq.32), kind=kOutput, calls=%fused_computation.7 | convolution fusion | flops 542375424 | bytes 3151873 | tf_op jit(solution)/shard_map/while/body/eval_jaxpr/dot_general | solution.py:32
  43.9 0.1 iota.6.clone
  44.0 29.4 %top_k.14 = (f32[512,512]{0,1:T(8,128)}, s32[512,512]{0,1:T(8,128)}) sort(f32[512,512]{0,1:T(8,128)S(1)} %get-tuple-element.42, s32[512,512]{0,1:T(8,128)S(1)} %iota.6.clone), dimensions={1}, to_apply=%region_0.1 | sort | flops 4718592 | bytes 4194304 | tf_op jit(solution)/shard_map/while/body/eval_jaxpr/top_k | solution.py:35
  73.4 1.6 %copy.16 = f32[512,512]{1,0:T(8,128)S(1)} copy(f32[512,512]{0,1:T(8,128)} %get-tuple-element.33) | data formatting | bytes 2097152 | tf_op jit(solution)/shard_map/while/body/eval_jaxpr/top_k | solution.py:35
  75.0 0.2 copy.11
  75.1 0.7 reshape.28
  75.8 6.8 %all-to-all-start = ((f32[16,1,320]{2,1,0:T(1,128)}), f32[16,1,320]{2,1,0:T(1,128)S(1)}, u32[]{:S(2)}, u32[]{:S(2)}) async-start(f32[16,1,320]{2,1,0:T(1,128)} %reshape.28), calls=%async_computation | async-start | bytes 49152 | tf_op jit(solution)/shard_map/all_to_all | solution.py:50
  82.7 42.1 %psum.7 = f32[512]{0:T(512)S(1)} all-reduce(f32[512]{0:T(512)S(1)} %get-tuple-element.41), channel_id=1, replica_groups=mesh['text'=16,'query'=2] {'text'}, use_global_device_ids=true, to_apply=%region_3.4 | all-reduce | flops 512 | bytes 4096 | tf_op jit(solution)/shard_map/psum | solution.py:52
  124.7 0.5 broadcast.12
  125.3 0.7 reduce.6
  126.0 0.1 reshape.29
  126.1 0.1 copy.12
  126.2 3.8 %top_k.20 = (f32[32,160]{1,0:T(8,128)S(1)}, s32[32,160]{1,0:T(8,128)}) sort(f32[32,160]{1,0:T(8,128)S(1)} %copy.12, s32[32,160]{1,0:T(8,128)S(1)} %iota.7), dimensions={1}, to_apply=%region_1.2 | sort | flops 66560 | bytes 81920 | tf_op jit(solution)/shard_map/top_k | solution.py:51
  130.0 0.2 slice_reduce_fusion.2
  130.1 0.7 copy.13
  130.8 0.1 subtract_bitcast_fusion.2
  130.9 0.6 pad_maximum_fusion
  (14 shorter events, 0.1 us)
Async XLA Ops:
  0.6 41.3 %copy-start = (bf16[512,1024]{1,0:T(8,128)(2,1)S(1)}, bf16[512,1024]{1,0:T(8,128)(2,1)}, u32[]{:S(2)}) copy-start(bf16[512,1024]{1,0:T(8,128)(2,1)} %param.6) | copy-start | bytes 3145732
  0.6 22.2 %copy-start.3 = (u32[32]{0:T(128)S(1)}, u32[32]{0:T(128)}, u32[]{:S(2)}) copy-start(u32[32]{0:T(128)} %constant.53) | copy-start | bytes 388
  0.7 23.5 %copy-start.2 = (s32[32]{0:T(128)S(1)}, s32[32]{0:T(128)}, u32[]{:S(2)}) copy-start(s32[32]{0:T(128)} %param.5) | copy-start | bytes 388
  0.7 41.3 %copy-start.1 = (s32[512]{0:T(512)S(1)}, s32[512]{0:T(512)}, u32[]{:S(2)}) copy-start(s32[512]{0:T(512)} %param.7) | copy-start | bytes 6148
  0.7 5.5 %collective-permute-start = (bf16[32,1024]{1,0:T(8,128)(2,1)}, bf16[32,1024]{1,0:T(8,128)(2,1)S(1)}, u32[]{:S(2)}, u32[]{:S(2)}) collective-permute-start(bf16[32,1024]{1,0:T(8,128)(2,1)} %param.4), channel_id=1, source_target_pairs={{0,2},{2,0},{4,6},{6,4},{8,10},{10,8},{12,14},{14,12},{16,18},{18,... | collective-permute-start | bytes 196616 | tf_op jit(solution)/shard_map/ppermute | solution.py:13
  7.1 5.1 %collective-permute-start.1 = (bf16[64,1024]{1,0:T(8,128)(2,1)S(1)}, bf16[64,1024]{1,0:T(8,128)(2,1)S(1)}, u32[]{:S(2)}, u32[]{:S(2)}) collective-permute-start(bf16[64,1024]{1,0:T(8,128)(2,1)S(1)} %maximum_select_fusion.4), channel_id=1, source_target_pairs={{0,4},{2,6},{4,0},{6,2},{8,12},{10,14},{12,8},{14,10},{16,20},{18,... | collective-permute-start | bytes 393224 | tf_op jit(solution)/shard_map/ppermute | solution.py:13
  12.2 6.5 %collective-permute-start.2 = (bf16[128,1024]{1,0:T(8,128)(2,1)S(1)}, bf16[128,1024]{1,0:T(8,128)(2,1)S(1)}, u32[]{:S(2)}, u32[]{:S(2)}) collective-permute-start(bf16[128,1024]{1,0:T(8,128)(2,1)S(1)} %maximum_select_fusion.3), channel_id=1, source_target_pairs={{0,8},{2,10},{4,12},{6,14},{8,0},{10,2},{12,4},{14,6},{16,24},{18,... | collective-permute-start | bytes 786440 | tf_op jit(solution)/shard_map/ppermute | solution.py:13
  18.9 23.1 %collective-permute-start.3 = (bf16[256,1024]{1,0:T(8,128)(2,1)S(1)}, bf16[256,1024]{1,0:T(8,128)(2,1)}, u32[]{:S(2)}, u32[]{:S(2)}) collective-permute-start(bf16[256,1024]{1,0:T(8,128)(2,1)S(1)} %maximum_select_fusion.2), channel_id=1, source_target_pairs={{0,16},{2,18},{4,20},{6,22},{8,24},{10,26},{12,28},{14,30},{16,0},... | collective-permute-start | bytes 1572872 | tf_op jit(solution)/shard_map/ppermute | solution.py:13
  75.8 48.9 %all-to-all-start = ((f32[16,1,320]{2,1,0:T(1,128)}), f32[16,1,320]{2,1,0:T(1,128)S(1)}, u32[]{:S(2)}, u32[]{:S(2)}) async-start(f32[16,1,320]{2,1,0:T(1,128)} %reshape.28), calls=%async_computation | async-start | bytes 49152 | tf_op jit(solution)/shard_map/all_to_all | solution.py:50
